TPU v7x, 32 devices: a whole 2x2x4 slice. The times are simulated.
32 devices in a mesh: dp: 4 (over y, x), mp: 8 (over z, core).
Axes of the slice: x: 2, y: 2, z: 4, core: 2. Of those that a mesh axis runs over, the one named last changes fastest.
Arguments:
- stored: float32 [16384, 18432], P(('dp', 'mp')), may hold values from -0.046875 to 0.046875
- row_map: int32 [16384], replicated, may hold values from 0 to 16383, as said below
- probe: bfloat16 [16384, 1024], P('dp'), may hold values from -6 to 6
- lane: bfloat16 [128, 1024], replicated, may hold values from -6 to 6
Outputs:
- shards: bfloat16 [144, 128, 16384], P('mp', None, 'dp')
- slab_checks: float32 [144, 32, 1024], P('mp', 'dp')
- head_sums: float32 [144, 1024], P('mp')
Inputs may be any that keep to these rules, and one draw needn't show every extreme that they name: row_map is a permutation of 0..16383 with row_map[i] // 4096 == (i % 512) // 128 for every stored row i.
All inputs are finite; a program needn't handle non-finite values.
Results may differ from a plain program's by a relative error of at most 0.0029.
Values may be sent and summed in bfloat16 or wider, within the bound.
A program may use at most 128 MiB of HBM per device.

v0:
```python
import functools

import jax
import jax.numpy as jnp
from jax import lax
from jax.experimental import pallas as pl
from jax.experimental.pallas import tpu as pltpu
from jax.sharding import PartitionSpec as P

Q_HEADS = 128
KV_HEADS = 8
HD = 128
SLABS = 8
PAIR = 2
AHEAD = 3
MESH = pl.DeviceIdType.MESH


def kernel(
    n_dp, n_mp, stored, local_row, probe, lane,
    shards, checks, heads, narrow, landing,
    onehot, wide, cast, arrived, turned, placed, slab_sums, sums,
    load_sem, local_sem, send_sem, recv_sem, out_sem, sum_send, sum_recv,
):
    my_dp = lax.axis_index("dp")
    my_mp = lax.axis_index("mp")
    n_dev = n_dp * n_mp
    me = my_dp * n_mp + my_mp
    rows_dev = stored.shape[0]
    sub = rows_dev // n_dp
    group_rows = probe.shape[0]
    slab_rows = group_rows // SLABS
    per_device = Q_HEADS // n_mp
    slots = per_device + 2
    share = n_mp // KV_HEADS
    chunks = slots // PAIR
    width = PAIR * HD

    barrier = pltpu.get_barrier_semaphore()

    def peer(k):
        return lax.rem(my_dp + k // n_mp, n_dp), lax.rem(my_mp + lax.rem(k, n_mp), n_mp)

    @pl.loop(1, n_dev)
    def _(k):
        pl.semaphore_signal(barrier, inc=1, device_id=peer(k), device_id_type=MESH)

    def load(step):
        copies = []
        for m in range(n_mp):
            if isinstance(step, int) and step == 0:
                for pos, head in enumerate((Q_HEADS + m // share, Q_HEADS + KV_HEADS + m // share)):
                    copies.append((stored.at[:, pl.ds(head * HD, HD)], wide.at[m, :, pl.ds(pos * HD, HD)]))
            else:
                first = pl.multiple_of((m * per_device + (step - 1) * PAIR) * HD, HD)
                copies.append((stored.at[:, pl.ds(first, width)], wide.at[m]))
        for src, dst in copies:
            pltpu.make_async_copy(src, dst, load_sem).start()
        pltpu.make_async_copy(wide, wide, load_sem).wait()

    def issue(step):
        load(step)

        @pl.loop(0, n_dp)
        def _(d):
            for m in range(n_mp):
                cast[d * n_mp + m] = wide[m, pl.ds(pl.multiple_of(d * sub, sub), sub), :].astype(jnp.bfloat16)

        to_narrow = pltpu.make_async_copy(cast, narrow.at[step], local_sem.at[0])
        own = pltpu.make_async_copy(cast.at[me], landing.at[step, me], local_sem.at[1])
        to_narrow.start()
        own.start()
        to_narrow.wait()
        own.wait()

        @pl.loop(1, n_dev)
        def _(k):
            dp, mp = peer(k)
            pltpu.make_async_remote_copy(
                src_ref=narrow.at[step, dp * n_mp + mp],
                dst_ref=landing.at[step, me],
                send_sem=send_sem.at[step],
                recv_sem=recv_sem.at[step],
                device_id=(dp, mp),
                device_id_type=MESH,
            ).start()

    pl.semaphore_wait(barrier, n_dev - 1)
    ahead = min(AHEAD, chunks)
    for step in range(ahead):
        issue(step)

    @pl.loop(0, SLABS)
    def _(i):
        rows = pl.ds(pl.multiple_of(i * slab_rows, slab_rows), slab_rows)
        target = local_row[rows, :]

        @pl.loop(0, SLABS)
        def _(j):
            first = pl.multiple_of(j * slab_rows, slab_rows)
            column = lax.broadcasted_iota(jnp.int32, (slab_rows, slab_rows), 1) + first
            onehot[rows, pl.ds(first, slab_rows)] = jnp.where(column == target, 1.0, 0.0).astype(jnp.bfloat16)

    group = max(1, HD // sub)
    span = group * sub

    def all_of(step):
        part = landing.at[step, pl.ds(0, n_dev - 1)]
        return pltpu.make_async_copy(part, part, recv_sem.at[step])

    def out_copy(first_slot):
        return pltpu.make_async_copy(placed, shards.at[pl.ds(first_slot, PAIR)], out_sem)

    @pl.loop(0, chunks)
    def _(step):
        first_slot = lax.rem(step * PAIR + per_device, slots)

        @pl.when(step + ahead < chunks)
        def _():
            issue(step + ahead)

        all_of(step).wait()
        fetch = pltpu.make_async_copy(landing.at[step], arrived, local_sem.at[0])
        fetch.start()
        fetch.wait()

        @pl.loop(0, n_dev // group)
        def _(b):
            rows = arrived[pl.ds(b * group, group)].astype(jnp.float32).reshape(span, width)
            turned[:, pl.ds(pl.multiple_of(b * span, span), span)] = rows.T.astype(jnp.bfloat16)

        @pl.when(step > 0)
        def _():
            out_copy(0).wait()

        @pl.loop(0, SLABS)
        def _(s):
            rows = pl.ds(pl.multiple_of(s * slab_rows, slab_rows), slab_rows)
            block = jnp.dot(turned[...], onehot[:, rows], preferred_element_type=jnp.float32).astype(jnp.bfloat16)
            placed[:, :, rows] = block.reshape(PAIR, HD, slab_rows)
            projected = jnp.dot(block, probe[rows, :], preferred_element_type=jnp.float32)
            weighted = projected.reshape(PAIR, HD, -1) * lane[...].astype(jnp.float32)[None]
            slab_sums[s] = jnp.sum(weighted, axis=1)

        out_copy(first_slot).start()
        for s in range(SLABS):
            for pos in range(PAIR):
                checks[first_slot + pos, s : s + 1, :] = slab_sums[s, pos : pos + 1, :]

    sums[my_dp] = jnp.sum(checks[...], axis=1)
    out_copy(0).wait()

    @pl.loop(1, n_dp)
    def _(k):
        pltpu.make_async_remote_copy(
            src_ref=sums.at[my_dp],
            dst_ref=sums.at[my_dp],
            send_sem=sum_send,
            recv_sem=sum_recv,
            device_id=(lax.rem(my_dp + k, n_dp), my_mp),
            device_id_type=MESH,
        ).start()

    others = sums.at[pl.ds(0, n_dp - 1)]
    pltpu.make_async_copy(others, others, sum_recv).wait()
    pltpu.make_async_copy(others, others, sum_send).wait()
    total = sums[0]
    for d in range(1, n_dp):
        total = total + sums[d]
    heads[...] = total / (n_dp * SLABS)

    @pl.loop(0, chunks)
    def _(step):
        part = narrow.at[step, pl.ds(0, n_dev - 1)]
        pltpu.make_async_copy(part, part, send_sem.at[step]).wait()


def body(stored, row_map, probe, lane):
    n_dp = lax.axis_size("dp")
    n_mp = lax.axis_size("mp")
    n_dev = n_dp * n_mp
    rows_dev, cols = stored.shape
    sub = rows_dev // n_dp
    group_rows, probes = probe.shape
    slots = Q_HEADS // n_mp + 2
    chunks = slots // PAIR
    width = PAIR * HD
    my_dp = lax.axis_index("dp")
    local_row = lax.dynamic_index_in_dim(row_map.reshape(n_dev, n_dp, sub), my_dp, 1, False)
    local_row = local_row.reshape(group_rows, 1) - my_dp * group_rows
    vmem = pl.BlockSpec(memory_space=pltpu.VMEM)
    hbm = pl.BlockSpec(memory_space=pl.ANY)
    moved = jax.ShapeDtypeStruct((chunks, n_dev, sub, width), jnp.bfloat16)
    shards, checks, heads, _, _ = pl.pallas_call(
        functools.partial(kernel, n_dp, n_mp),
        out_shape=(
            jax.ShapeDtypeStruct((slots, HD, group_rows), jnp.bfloat16),
            jax.ShapeDtypeStruct((slots, SLABS, probes), jnp.float32),
            jax.ShapeDtypeStruct((slots, probes), jnp.float32),
            moved,
            moved,
        ),
        in_specs=[hbm, vmem, vmem, vmem],
        out_specs=(hbm, vmem, vmem, hbm, hbm),
        scratch_shapes=[
            pltpu.VMEM((group_rows, group_rows), jnp.bfloat16),
            pltpu.VMEM((n_mp, rows_dev, width), jnp.float32),
            pltpu.VMEM((n_dev, sub, width), jnp.bfloat16),
            pltpu.VMEM((n_dev, sub, width), jnp.bfloat16),
            pltpu.VMEM((width, group_rows), jnp.bfloat16),
            pltpu.VMEM((PAIR, HD, group_rows), jnp.bfloat16),
            pltpu.VMEM((SLABS, PAIR, probes), jnp.float32),
            pltpu.VMEM((n_dp, slots, probes), jnp.float32),
            pltpu.SemaphoreType.DMA,
            pltpu.SemaphoreType.DMA((2,)),
            pltpu.SemaphoreType.DMA((chunks,)),
            pltpu.SemaphoreType.DMA((chunks,)),
            pltpu.SemaphoreType.DMA,
            pltpu.SemaphoreType.DMA,
            pltpu.SemaphoreType.DMA,
        ],
        compiler_params=pltpu.CompilerParams(
            collective_id=0, has_side_effects=True, vmem_limit_bytes=66_000_000
        ),
    )(stored, local_row, probe, lane)
    return shards, checks, heads


def solution(mesh):
    return jax.shard_map(
        body,
        mesh=mesh,
        in_specs=(P(("dp", "mp"), None), P(), P("dp", None), P()),
        out_specs=(P("mp", None, "dp"), P("mp", "dp", None), P("mp", None)),
        check_vma=False,
    )
```

profile of v0, /device:TPU:0, one launch (start us, length us, event | category | flops | bytes accessed | tf_op | source)
XLA Modules:
  0.0 472.7 jit_solution(14803535339869363853)
XLA Ops:
  0.6 0.9 subtract_bitcast_fusion
  1.5 2.0 copy.7.local_row
  3.5 450.9 %shard_map.67 = (bf16[18,128,4096]{2,1,0:T(8,128)(2,1)}, f32[18,8,1024]{2,1,0:T(8,128)}, f32[18,1024]{1,0:T(8,128)}, bf16[9,32,128,256]{3,2,1,0:T(8,128)(2,1)}, bf16[9,32,128,256]{3,2,1,0:T(8,128)(2,1)}) custom-call(f32[512,18432]{1,0:T(8,128)} %stored.1, s32[4096,1]{1,0:T(8,128)} %copy.7.local_row, bf16[4096,1024]{1,0:T(8,128)(2,1)} %probe.1, ...), custom_call_target="tpu_custom_call" | custom-call | tf_op jit(solution)/shard_map/pallas_call | solution.py:194
  454.4 0.0 copy-start
  454.4 0.0 copy-start.1
  454.4 16.8 %copy.11 = bf16[18,128,4096]{2,1,0:T(8,128)(2,1)} copy(bf16[18,128,4096]{2,1,0:T(8,128)(2,1)} %get-tuple-element.12) | data formatting | bytes 37748736
  471.2 0.0 copy-done
  471.2 0.8 copy.12
  472.0 0.0 copy-done.1
  472.0 0.6 copy.13
Async XLA Ops:
  454.4 16.9 %copy-start = (f32[18,8,1024]{2,1,0:T(8,128)S(1)}, f32[18,8,1024]{2,1,0:T(8,128)}, u32[]{:S(2)}) copy-start(f32[18,8,1024]{2,1,0:T(8,128)} %get-tuple-element.13) | copy-start | bytes 1769476
  454.4 17.7 %copy-start.1 = (f32[18,1024]{1,0:T(8,128)S(1)}, f32[18,1024]{1,0:T(8,128)}, u32[]{:S(2)}) copy-start(f32[18,1024]{1,0:T(8,128)} %get-tuple-element.14) | copy-start | bytes 221188
where the time goes:
time: 475 us; the launch traced here: 473 us
  Pallas kernels  451 us (95%)
  local copies, waits for them, and re-layouts  20.3 us (4%)
    pallas_call x1, Pallas kernels, body(): pl.pallas_call(functools.partial(kernel, n_dp, n_mp), out_shape=(jax.Shap...  451 us
    unnamed x7, local copies, waits for them, and re-layouts  18.3 us

commit v1 on v0

v1 whole, which is shorter than its diff:
```python
import functools

import jax
import jax.numpy as jnp
from jax import lax
from jax.experimental import pallas as pl
from jax.experimental.pallas import tpu as pltpu
from jax.sharding import PartitionSpec as P

Q_HEADS = 128
KV_HEADS = 8
HD = 128
SLABS = 8
PAIR = 2
AHEAD = 3
UNROLL = 4
MESH = pl.DeviceIdType.MESH


def exchange(
    n_dp, n_mp, stored, row_map, probe_any, lane_any,
    shards, checks, heads, landing,
    narrow, wide, bufs, turned, acc, probe, lane, table, offset, slab_sums, sums, tail_sums,
    load_sem, aux_sem, fetch_sem, send_sem, recv_sem, sum_send, sum_recv, tail_send, tail_recv,
):
    my_dp = lax.axis_index("dp")
    my_mp = lax.axis_index("mp")
    n_dev = n_dp * n_mp
    rows_dev = stored.shape[0]
    sub = rows_dev // n_dp
    group_rows = probe.shape[0]
    slab_rows = group_rows // SLABS
    per_device = Q_HEADS // n_mp
    slots = per_device + 2
    share = n_mp // KV_HEADS
    chunks = slots // PAIR
    last = chunks - 1
    width = PAIR * HD
    half = n_mp // 2
    my_half = my_mp // half
    part_rows = n_dp * sub
    ahead = min(AHEAD, chunks)
    last_slot = (last * PAIR + per_device) % slots

    def peer_mp(i):
        other = i // half
        side = (1 - my_half) * (1 - other) + my_half * other
        return side * half + lax.rem(my_mp + i, half)

    def group_mp(i):
        far = i // half
        inner = lax.rem(i, half)
        own = my_half * half + lax.rem(my_mp + inner, half)
        other = my_half * inner + (1 - my_half) * (n_mp - 1 - inner)
        return own * (1 - far) + other * far

    def load(step, i):
        mp = peer_mp(i)
        if isinstance(step, int) and step == 0:
            for pos, head in enumerate((Q_HEADS + mp // share, Q_HEADS + KV_HEADS + mp // share)):
                first = pl.multiple_of(head * HD, HD)
                src = stored.at[:, pl.ds(first, HD)]
                pltpu.make_async_copy(src, wide.at[i, :, pl.ds(pos * HD, HD)], load_sem.at[i]).start()
        else:
            first = pl.multiple_of((mp * per_device + (step - 1) * PAIR) * HD, HD)
            pltpu.make_async_copy(stored.at[:, pl.ds(first, width)], wide.at[i], load_sem.at[i]).start()

    def issue(step):
        @pl.loop(0, n_mp)
        def _(i):
            mp = peer_mp(i)
            pltpu.make_async_copy(wide.at[i], wide.at[i], load_sem.at[i]).wait()

            @pl.loop(0, n_dp)
            def _(d):
                narrow[step, mp, d] = wide[i, pl.ds(pl.multiple_of(d * sub, sub), sub), :].astype(jnp.bfloat16)

            @pl.loop(0, n_dp)
            def _(a):
                @pl.when(i * n_dp + a != half * n_dp)
                def _():
                    dp = lax.rem(my_dp + a, n_dp)

                    def send(target):
                        pltpu.make_async_remote_copy(
                            src_ref=narrow.at[step, mp, dp],
                            dst_ref=target,
                            send_sem=send_sem.at[step],
                            recv_sem=recv_sem.at[step, my_mp],
                            device_id=(dp, mp),
                            device_id_type=MESH,
                        ).start()

                    if isinstance(step, int):
                        send(bufs.at[1, my_mp, my_dp] if step == last else landing.at[step, my_mp, my_dp])
                    else:
                        @pl.when(step < last)
                        def _():
                            send(landing.at[step, my_mp, my_dp])

                        @pl.when(step == last)
                        def _():
                            send(bufs.at[1, my_mp, my_dp])

            if isinstance(step, int):
                if step < last:
                    load(step + 1, i)
            else:
                @pl.when(step < last)
                def _():
                    load(step + 1, i)

    @pl.loop(0, n_mp)
    def _(i):
        load(0, i)

    barrier = pltpu.get_barrier_semaphore()

    @pl.loop(1, n_dev)
    def _(k):
        other = (lax.rem(my_dp + k // n_mp, n_dp), lax.rem(my_mp + lax.rem(k, n_mp), n_mp))
        pl.semaphore_signal(barrier, inc=1, device_id=other, device_id_type=MESH)

    aux = (
        pltpu.make_async_copy(row_map, table, aux_sem.at[0]),
        pltpu.make_async_copy(lane_any, lane, aux_sem.at[1]),
        pltpu.make_async_copy(probe_any, probe, aux_sem.at[2]),
    )
    pl.semaphore_wait(barrier, n_dev - 1)
    issue(0)
    for copy in aux:
        copy.start()
    for step in range(1, ahead):
        issue(step)

    for copy in aux:
        copy.wait()
    diagonal = lax.broadcasted_iota(jnp.int32, (sub, sub), 0) == lax.broadcasted_iota(jnp.int32, (sub, sub), 1)
    lanes = lax.broadcasted_iota(jnp.int32, (sub, HD), 1)

    @pl.loop(0, n_mp)
    def _(mp):
        @pl.loop(0, n_dp)
        def _(dp):
            row = table[dp * n_mp + mp, pl.ds(my_dp, 1), :].astype(jnp.float32)
            column = jnp.sum(jnp.where(diagonal, row, 0.0), axis=1, keepdims=True).astype(jnp.int32)
            offset[mp, pl.ds(pl.multiple_of(dp * sub, sub), sub), :] = column - my_dp * group_rows - lanes

    acc[...] = jnp.zeros_like(acc)
    checks[last_slot : last_slot + PAIR] = jnp.zeros((PAIR,) + checks.shape[1:], jnp.float32)
    pieces = max(1, HD // sub)
    span = pieces * sub

    def arrival(step, mp):
        whole = landing.at[0, 0]
        return pltpu.make_async_copy(whole, whole, recv_sem.at[step, mp])

    def own_arrival(step):
        if n_dp > 1:
            part = landing.at[0, 0, pl.ds(0, n_dp - 1)]
            pltpu.make_async_copy(part, part, recv_sem.at[step, my_mp]).wait()

    @pl.loop(0, chunks)
    def _(step):
        first_slot = lax.rem(step * PAIR + per_device, slots)
        slot = step // last

        @pl.when(step + ahead < chunks)
        def _():
            issue(step + ahead)

        @pl.when(step < last)
        def _():
            own_arrival(step)

            @pl.loop(1, n_mp)
            def _(i):
                arrival(step, group_mp(i)).wait()

            fetch = pltpu.make_async_copy(landing.at[step], bufs.at[0], fetch_sem)
            fetch.start()
            fetch.wait()

        @pl.when(step == last)
        def _():
            sums[my_dp] = jnp.sum(checks[...], axis=1)

            @pl.loop(1, n_dp)
            def _(k):
                pltpu.make_async_remote_copy(
                    src_ref=sums.at[my_dp],
                    dst_ref=sums.at[my_dp],
                    send_sem=sum_send,
                    recv_sem=sum_recv,
                    device_id=(lax.rem(my_dp + k, n_dp), my_mp),
                    device_id_type=MESH,
                ).start()

            own_arrival(last)

        bufs[slot, my_mp, my_dp] = narrow[step, my_mp, my_dp]

        @pl.loop(0, n_mp)
        def _(i):
            mp = group_mp(i)

            @pl.when(slot * i > 0)
            def _():
                arrival(last, mp).wait()

            for b in range(n_dp // pieces):
                rows = bufs[slot, mp, pl.ds(b * pieces, pieces)].astype(jnp.float32).reshape(span, width)
                turned[:, pl.ds(b * span, span)] = rows.T.astype(jnp.bfloat16)

            @pl.loop(0, SLABS // UNROLL)
            def _(j):
                for u in range(UNROLL):
                    first = pl.multiple_of((j * UNROLL + u) * slab_rows, slab_rows)
                    marks = [
                        jnp.where(offset[mp] == first + t * HD, 1.0, 0.0).astype(jnp.bfloat16)
                        for t in range(slab_rows // HD)
                    ]
                    onehot = jnp.concatenate(marks, axis=1)
                    cols = pl.ds(first, slab_rows)
                    acc[:, cols] += jnp.dot(turned[...], onehot, preferred_element_type=jnp.float32)

        @pl.loop(0, SLABS)
        def _(s):
            rows = pl.ds(pl.multiple_of(s * slab_rows, slab_rows), slab_rows)
            block = acc[:, rows].astype(jnp.bfloat16)
            acc[:, rows] = jnp.zeros((width, slab_rows), jnp.float32)
            shards[pl.ds(first_slot, PAIR), :, rows] = block.reshape(PAIR, HD, slab_rows)
            projected = jnp.dot(block, probe[rows, :], preferred_element_type=jnp.float32)
            weighted = projected.reshape(PAIR, HD, -1) * lane[...].astype(jnp.float32)[None]
            slab_sums[s] = jnp.sum(weighted, axis=1)

        for s in range(SLABS):
            for pos in range(PAIR):
                checks[first_slot + pos, s : s + 1, :] = slab_sums[s, pos : pos + 1, :]

    tail_sums[my_dp, :PAIR] = jnp.sum(checks[last_slot : last_slot + PAIR], axis=1)

    @pl.loop(1, n_dp)
    def _(k):
        pltpu.make_async_remote_copy(
            src_ref=tail_sums.at[my_dp],
            dst_ref=tail_sums.at[my_dp],
            send_sem=tail_send,
            recv_sem=tail_recv,
            device_id=(lax.rem(my_dp + k, n_dp), my_mp),
            device_id_type=MESH,
        ).start()

    @pl.loop(0, chunks)
    def _(step):
        @pl.when(step >= 0)
        def _():
            part = narrow.at[0, 0]
            for m in range(n_mp - 1):
                pltpu.make_async_copy(part, part, send_sem.at[step]).wait()
            if n_dp > 1:
                part = narrow.at[0, 0, pl.ds(0, n_dp - 1)]
                pltpu.make_async_copy(part, part, send_sem.at[step]).wait()

    for buf, send, recv in ((sums, sum_send, sum_recv), (tail_sums, tail_send, tail_recv)):
        others = buf.at[pl.ds(0, n_dp - 1)]
        pltpu.make_async_copy(others, others, recv).wait()
        pltpu.make_async_copy(others, others, send).wait()
    total = sums[0]
    tail = tail_sums[0]
    for d in range(1, n_dp):
        total = total + sums[d]
        tail = tail + tail_sums[d]
    heads[...] = total / (n_dp * SLABS)
    heads[last_slot : last_slot + PAIR] = tail[:PAIR] / (n_dp * SLABS)


def write_out(shards, checks, heads, shards_out, checks_out, heads_out, sems):
    copies = [
        pltpu.make_async_copy(shards.at[h], shards_out.at[h], sems.at[h]) for h in range(shards.shape[0])
    ]
    copies.append(pltpu.make_async_copy(checks, checks_out, sems.at[shards.shape[0]]))
    copies.append(pltpu.make_async_copy(heads, heads_out, sems.at[shards.shape[0] + 1]))
    for copy in copies:
        copy.start()
    for copy in copies:
        copy.wait()


def body(stored, row_map, probe, lane):
    n_dp = lax.axis_size("dp")
    n_mp = lax.axis_size("mp")
    n_dev = n_dp * n_mp
    rows_dev = stored.shape[0]
    sub = rows_dev // n_dp
    group_rows, probes = probe.shape
    slots = Q_HEADS // n_mp + 2
    chunks = slots // PAIR
    width = PAIR * HD
    vmem = pl.BlockSpec(memory_space=pltpu.VMEM)
    hbm = pl.BlockSpec(memory_space=pl.ANY)
    shapes = (
        ((slots, HD, group_rows), jnp.bfloat16),
        ((slots, SLABS, probes), jnp.float32),
        ((slots, probes), jnp.float32),
    )
    kept = pl.pallas_call(
        functools.partial(exchange, n_dp, n_mp),
        out_shape=tuple(pltpu.VMEM(*s) for s in shapes)
        + (jax.ShapeDtypeStruct((chunks, n_mp, n_dp, sub, width), jnp.bfloat16),),
        in_specs=[hbm, hbm, hbm, hbm],
        out_specs=(vmem, vmem, vmem, hbm),
        scratch_shapes=[
            pltpu.VMEM((chunks, n_mp, n_dp, sub, width), jnp.bfloat16),
            pltpu.VMEM((n_mp, rows_dev, width), jnp.float32),
            pltpu.VMEM((2, n_mp, n_dp, sub, width), jnp.bfloat16),
            pltpu.VMEM((width, n_dp * sub), jnp.bfloat16),
            pltpu.VMEM((width, group_rows), jnp.float32),
            pltpu.VMEM((group_rows, probes), jnp.bfloat16),
            pltpu.VMEM(lane.shape, jnp.bfloat16),
            pltpu.VMEM((n_dev, n_dp, sub), jnp.int32),
            pltpu.VMEM((n_mp, n_dp * sub, HD), jnp.int32),
            pltpu.VMEM((SLABS, PAIR, probes), jnp.float32),
            pltpu.VMEM((n_dp, slots, probes), jnp.float32),
            pltpu.VMEM((n_dp, 8, probes), jnp.float32),
            pltpu.SemaphoreType.DMA((n_mp,)),
            pltpu.SemaphoreType.DMA((3,)),
            pltpu.SemaphoreType.DMA,
            pltpu.SemaphoreType.DMA((chunks,)),
            pltpu.SemaphoreType.DMA((chunks, n_mp)),
            pltpu.SemaphoreType.DMA,
            pltpu.SemaphoreType.DMA,
            pltpu.SemaphoreType.DMA,
            pltpu.SemaphoreType.DMA,
        ],
        compiler_params=pltpu.CompilerParams(
            collective_id=0, has_side_effects=True, vmem_limit_bytes=47_000_000
        ),
    )(stored, row_map.reshape(n_dev, n_dp, sub), probe, lane)
    return pl.pallas_call(
        write_out,
        out_shape=tuple(jax.ShapeDtypeStruct(*s) for s in shapes),
        in_specs=[vmem, vmem, vmem],
        out_specs=(hbm, hbm, hbm),
        scratch_shapes=[pltpu.SemaphoreType.DMA((slots + 2,))],
        compiler_params=pltpu.CompilerParams(vmem_limit_bytes=1_000_000),
    )(*kept[:3])


def solution(mesh):
    return jax.shard_map(
        body,
        mesh=mesh,
        in_specs=(P(("dp", "mp"), None), P(), P("dp", None), P()),
        out_specs=(P("mp", None, "dp"), P("mp", "dp", None), P("mp", None)),
        check_vma=False,
    )
```

time: 475 us -> 441 us (0.928)
  local copies, waits for them, and re-layouts: 20.3 us -> 0 us
  Pallas kernels: 451 us -> 440 us
    unnamed x7 -> x0, local copies, waits for them, and re-layouts: 18.3 us -> none
    pallas_call x1 -> x2, Pallas kernels: 451 us -> 440 us  [the longest x1 433 us: body(): pl.pallas_call(functools.partial(exchange, n_dp, n_mp), out_shape=tuple((...]
where the time goes in v1:
time: 441 us; the launch traced here: 440 us
  Pallas kernels  440 us (100%)
    pallas_call x1, Pallas kernels, body(): pl.pallas_call(functools.partial(exchange, n_dp, n_mp), out_shape=tuple((...  433 us

profile of v1, /device:TPU:0, one launch (start us, length us, event | category | flops | bytes accessed | tf_op | source)
XLA Modules:
  0.0 440.4 jit_solution(17510410767391573502)
XLA Ops:
  0.6 433.0 %shard_map.67 = (bf16[18,128,4096]{2,1,0:T(8,128)(2,1)S(1)}, f32[18,8,1024]{2,1,0:T(8,128)S(1)}, f32[18,1024]{1,0:T(8,128)S(1)}, bf16[9,8,4,128,256]{4,3,2,1,0:T(8,128)(2,1)}) custom-call(f32[512,18432]{1,0:T(8,128)} %stored.1, s32[32,4,128]{2,1,0:T(4,128)} %bitcast.1, bf16[4096,1024]{1,0:T(8,128)(2,1)} %probe_any.1, bf16[128,1024]{1,0:T(8,128)(2,1)} %lane_any.1), custom_call_target="tpu_custom_call" | custom-call | tf_op jit(solution)/shard_map/pallas_call | solution.py:307
  433.6 6.8 %shard_map.68 = (bf16[18,128,4096]{2,1,0:T(8,128)(2,1)}, f32[18,8,1024]{2,1,0:T(8,128)}, f32[18,1024]{1,0:T(8,128)}) custom-call(bf16[18,128,4096]{2,1,0:T(8,128)(2,1)S(1)} %get-tuple-element.6.shards, f32[18,8,1024]{2,1,0:T(8,128)S(1)} %get-tuple-element.7.checks, f32[18,1024]{1,0:T(8,128)S(1)} %get-tuple-element.8.heads), custom_call_target="tpu_custom_call" | custom-call | tf_op jit(solution)/shard_map/pallas_call | solution.py:340

commit v2 on v1

--- a/solution.py
+++ b/solution.py
@@ -14,14 +14,17 @@
 PAIR = 2
 AHEAD = 3
 UNROLL = 4
+FINAL = 2
+PROBE_COLS = 256
 MESH = pl.DeviceIdType.MESH
 
 
 def exchange(
     n_dp, n_mp, stored, row_map, probe_any, lane_any,
     shards, checks, heads, landing,
-    narrow, wide, bufs, turned, acc, probe, lane, table, offset, slab_sums, sums, tail_sums,
-    load_sem, aux_sem, fetch_sem, send_sem, recv_sem, sum_send, sum_recv, tail_send, tail_recv,
+    narrow, wide, bufs, turned, probe, lane, table, offset, late_turned, late_offset, late_onehot,
+    slab_sums, sums, tail_sums,
+    load_sem, aux_sem, fetch_sem, send_sem, recv_sem, late_sem, sum_send, sum_recv, tail_send, tail_recv,
 ):
     my_dp = lax.axis_index("dp")
     my_mp = lax.axis_index("mp")
@@ -41,6 +44,14 @@
     part_rows = n_dp * sub
     ahead = min(AHEAD, chunks)
     last_slot = (last * PAIR + per_device) % slots
+    near = half // 2
+    pieces = max(1, HD // sub)
+    span = pieces * sub
+    late_each = max(1, HD // (near * sub))
+    late_groups = n_dp // late_each
+
+    quarter = my_mp // near
+    middle = quarter * (3 - quarter) // 2
 
     def peer_mp(i):
         other = i // half
@@ -65,6 +76,43 @@
             first = pl.multiple_of((mp * per_device + (step - 1) * PAIR) * HD, HD)
             pltpu.make_async_copy(stored.at[:, pl.ds(first, width)], wide.at[i], load_sem.at[i]).start()
 
+    def send(step, mp, dp, target, arrived):
+        pltpu.make_async_remote_copy(
+            src_ref=narrow.at[step, mp, dp],
+            dst_ref=target,
+            send_sem=send_sem.at[step],
+            recv_sem=arrived,
+            device_id=(dp, mp),
+            device_id_type=MESH,
+        ).start()
+
+    def send_all(step, i):
+        @pl.loop(0, n_dp)
+        def _(a):
+            @pl.when(i * n_dp + a != half * n_dp)
+            def _():
+                dp = lax.rem(my_dp + a, n_dp)
+                send(step, peer_mp(i), dp, landing.at[step, my_mp, my_dp], recv_sem.at[step, my_mp])
+
+    def send_last():
+        @pl.loop(0, n_dp)
+        def _(a):
+            dp = lax.rem(my_dp + a, n_dp)
+
+            @pl.loop(0, n_mp)
+            def _(i):
+                late = middle * (1 - i // half)
+
+                @pl.when(late == 1)
+                def _():
+                    send(last, peer_mp(i), dp, bufs.at[1, my_mp, my_dp], late_sem.at[a // late_each])
+
+                @pl.when(late == 0)
+                def _():
+                    @pl.when(i * n_dp + a != half * n_dp)
+                    def _():
+                        send(last, peer_mp(i), dp, bufs.at[1, my_mp, my_dp], recv_sem.at[last, my_mp])
+
     def issue(step):
         @pl.loop(0, n_mp)
         def _(i):
@@ -75,32 +123,12 @@
             def _(d):
                 narrow[step, mp, d] = wide[i, pl.ds(pl.multiple_of(d * sub, sub), sub), :].astype(jnp.bfloat16)
 
-            @pl.loop(0, n_dp)
-            def _(a):
-                @pl.when(i * n_dp + a != half * n_dp)
+            if not isinstance(step, int):
+                @pl.when(step < last)
                 def _():
-                    dp = lax.rem(my_dp + a, n_dp)
-
-                    def send(target):
-                        pltpu.make_async_remote_copy(
-                            src_ref=narrow.at[step, mp, dp],
-                            dst_ref=target,
-                            send_sem=send_sem.at[step],
-                            recv_sem=recv_sem.at[step, my_mp],
-                            device_id=(dp, mp),
-                            device_id_type=MESH,
-                        ).start()
-
-                    if isinstance(step, int):
-                        send(bufs.at[1, my_mp, my_dp] if step == last else landing.at[step, my_mp, my_dp])
-                    else:
-                        @pl.when(step < last)
-                        def _():
-                            send(landing.at[step, my_mp, my_dp])
-
-                        @pl.when(step == last)
-                        def _():
-                            send(bufs.at[1, my_mp, my_dp])
+                    send_all(step, i)
+            elif step < last:
+                send_all(step, i)
 
             if isinstance(step, int):
                 if step < last:
@@ -109,6 +137,14 @@
                 @pl.when(step < last)
                 def _():
                     load(step + 1, i)
+
+        if isinstance(step, int):
+            if step == last:
+                send_last()
+        else:
+            @pl.when(step == last)
+            def _():
+                send_last()
 
     @pl.loop(0, n_mp)
     def _(i):
@@ -146,10 +182,65 @@
             column = jnp.sum(jnp.where(diagonal, row, 0.0), axis=1, keepdims=True).astype(jnp.int32)
             offset[mp, pl.ds(pl.multiple_of(dp * sub, sub), sub), :] = column - my_dp * group_rows - lanes
 
-    acc[...] = jnp.zeros_like(acc)
-    checks[last_slot : last_slot + PAIR] = jnp.zeros((PAIR,) + checks.shape[1:], jnp.float32)
-    pieces = max(1, HD // sub)
-    span = pieces * sub
+    def late_pieces(g):
+        side = (1 - my_half) * half
+        inner = my_half * near
+        for k in range(late_each):
+            dp = lax.rem(my_dp + n_dp - (g * late_each + k), n_dp)
+            for m in range(near):
+                yield side + inner + m, dp
+
+    @pl.loop(0, late_groups)
+    def _(g):
+        for k, (mp, dp) in enumerate(late_pieces(g)):
+            late_offset[g, k * sub : (k + 1) * sub, :] = offset[mp, pl.ds(pl.multiple_of(dp * sub, sub), sub), :]
+
+    def onehot(numbers, first):
+        marks = [
+            jnp.where(numbers == first + t * HD, 1.0, 0.0).astype(jnp.bfloat16) for t in range(slab_rows // HD)
+        ]
+        return jnp.concatenate(marks, axis=1)
+
+    @pl.loop(0, SLABS)
+    def _(s):
+        first = pl.multiple_of(s * slab_rows, slab_rows)
+        late_onehot[:, pl.ds(first, slab_rows)] = onehot(late_offset[late_groups - 1], first)
+
+    def turn(slot, mp):
+        for b in range(n_dp // pieces):
+            rows = bufs[slot, mp, pl.ds(b * pieces, pieces)].astype(jnp.float32).reshape(span, width)
+            turned[:, pl.ds(b * span, span)] = rows.T.astype(jnp.bfloat16)
+
+    def turn_late(g):
+        rows = [bufs[1, mp, dp].astype(jnp.float32) for mp, dp in late_pieces(g)]
+        late_turned[...] = jnp.concatenate(rows, axis=0).T.astype(jnp.bfloat16)
+
+    def place(values, numbers, first_slot):
+        @pl.loop(0, SLABS // UNROLL)
+        def _(j):
+            for u in range(UNROLL):
+                first = pl.multiple_of((j * UNROLL + u) * slab_rows, slab_rows)
+                cols = pl.ds(first, slab_rows)
+                found = jnp.dot(values[...], onehot(numbers[...], first), preferred_element_type=jnp.float32)
+                held = pl.ds(first_slot, PAIR)
+                shards[held, :, cols] += found.astype(jnp.bfloat16).reshape(PAIR, HD, slab_rows)
+
+    def finish(s, block):
+        rows = pl.ds(pl.multiple_of(s * slab_rows, slab_rows), slab_rows)
+        for p in range(0, probe.shape[1], PROBE_COLS):
+            cols = slice(p, p + PROBE_COLS)
+            projected = jnp.dot(block, probe[rows, cols], preferred_element_type=jnp.float32)
+            weighted = projected.reshape(PAIR, HD, -1) * lane[:, cols].astype(jnp.float32)[None]
+            slab_sums[s, :, cols] = jnp.sum(weighted, axis=1)
+
+    def store_checks(first_slot):
+        for s in range(SLABS):
+            for pos in range(PAIR):
+                checks[first_slot + pos, s : s + 1, :] = slab_sums[s, pos : pos + 1, :]
+
+    @pl.loop(0, slots)
+    def _(h):
+        shards[h] = jnp.zeros(shards.shape[1:], jnp.bfloat16)
 
     def arrival(step, mp):
         whole = landing.at[0, 0]
@@ -160,84 +251,106 @@
             part = landing.at[0, 0, pl.ds(0, n_dp - 1)]
             pltpu.make_async_copy(part, part, recv_sem.at[step, my_mp]).wait()
 
-    @pl.loop(0, chunks)
+    def slot_of(step):
+        return lax.rem(step * PAIR + per_device, slots)
+
+    def take(step, low, high):
+        @pl.loop(low, high)
+        def _(i):
+            mp = group_mp(i)
+
+            @pl.when(i > 0)
+            def _():
+                arrival(step, mp).wait()
+
+            @pl.when(i == 0)
+            def _():
+                own_arrival(step)
+
+        @pl.when(step < last)
+        def _():
+            @pl.loop(low, high)
+            def _(i):
+                mp = group_mp(i)
+                pltpu.make_async_copy(landing.at[step, mp], bufs.at[0, mp], fetch_sem).start()
+
+            part = landing.at[0, pl.ds(0, high - low)]
+            pltpu.make_async_copy(part, part, fetch_sem).wait()
+
+    def put(step, low, high):
+        slot = step // last
+
+        @pl.loop(low, high)
+        def _(i):
+            mp = group_mp(i)
+            turn(slot, mp)
+            place(turned, offset.at[mp], slot_of(step))
+
+    def early(step):
+        take(step, 0, n_mp - near)
+        bufs[step // last, my_mp, my_dp] = narrow[step, my_mp, my_dp]
+        put(step, 0, n_mp - near)
+
+    early(0)
+
+    @pl.loop(0, last)
     def _(step):
-        first_slot = lax.rem(step * PAIR + per_device, slots)
-        slot = step // last
-
         @pl.when(step + ahead < chunks)
         def _():
             issue(step + ahead)
 
-        @pl.when(step < last)
-        def _():
-            own_arrival(step)
-
-            @pl.loop(1, n_mp)
-            def _(i):
-                arrival(step, group_mp(i)).wait()
-
-            fetch = pltpu.make_async_copy(landing.at[step], bufs.at[0], fetch_sem)
-            fetch.start()
-            fetch.wait()
-
-        @pl.when(step == last)
-        def _():
-            sums[my_dp] = jnp.sum(checks[...], axis=1)
-
-            @pl.loop(1, n_dp)
-            def _(k):
-                pltpu.make_async_remote_copy(
-                    src_ref=sums.at[my_dp],
-                    dst_ref=sums.at[my_dp],
-                    send_sem=sum_send,
-                    recv_sem=sum_recv,
-                    device_id=(lax.rem(my_dp + k, n_dp), my_mp),
-                    device_id_type=MESH,
-                ).start()
-
-            own_arrival(last)
-
-        bufs[slot, my_mp, my_dp] = narrow[step, my_mp, my_dp]
-
-        @pl.loop(0, n_mp)
-        def _(i):
-            mp = group_mp(i)
-
-            @pl.when(slot * i > 0)
-            def _():
-                arrival(last, mp).wait()
-
-            for b in range(n_dp // pieces):
-                rows = bufs[slot, mp, pl.ds(b * pieces, pieces)].astype(jnp.float32).reshape(span, width)
-                turned[:, pl.ds(b * span, span)] = rows.T.astype(jnp.bfloat16)
-
-            @pl.loop(0, SLABS // UNROLL)
-            def _(j):
-                for u in range(UNROLL):
-                    first = pl.multiple_of((j * UNROLL + u) * slab_rows, slab_rows)
-                    marks = [
-                        jnp.where(offset[mp] == first + t * HD, 1.0, 0.0).astype(jnp.bfloat16)
-                        for t in range(slab_rows // HD)
-                    ]
-                    onehot = jnp.concatenate(marks, axis=1)
-                    cols = pl.ds(first, slab_rows)
-                    acc[:, cols] += jnp.dot(turned[...], onehot, preferred_element_type=jnp.float32)
-
-        @pl.loop(0, SLABS)
-        def _(s):
-            rows = pl.ds(pl.multiple_of(s * slab_rows, slab_rows), slab_rows)
-            block = acc[:, rows].astype(jnp.bfloat16)
-            acc[:, rows] = jnp.zeros((width, slab_rows), jnp.float32)
-            shards[pl.ds(first_slot, PAIR), :, rows] = block.reshape(PAIR, HD, slab_rows)
-            projected = jnp.dot(block, probe[rows, :], preferred_element_type=jnp.float32)
-            weighted = projected.reshape(PAIR, HD, -1) * lane[...].astype(jnp.float32)[None]
-            slab_sums[s] = jnp.sum(weighted, axis=1)
-
-        for s in range(SLABS):
-            for pos in range(PAIR):
-                checks[first_slot + pos, s : s + 1, :] = slab_sums[s, pos : pos + 1, :]
-
+        early(step + 1)
+        take(step, n_mp - near, n_mp)
+        put(step, n_mp - near, n_mp)
+        first_slot = slot_of(step)
+
+        @pl.loop(0, SLABS // FINAL)
+        def _(j):
+            for u in range(FINAL):
+                s = j * FINAL + u
+                cols = pl.ds(pl.multiple_of(s * slab_rows, slab_rows), slab_rows)
+                finish(s, shards[pl.ds(first_slot, PAIR), :, cols].reshape(width, slab_rows))
+
+        store_checks(first_slot)
+
+    checks[last_slot : last_slot + PAIR] = jnp.zeros((PAIR,) + checks.shape[1:], jnp.float32)
+    sums[my_dp] = jnp.sum(checks[...], axis=1)
+
+    @pl.loop(1, n_dp)
+    def _(k):
+        pltpu.make_async_remote_copy(
+            src_ref=sums.at[my_dp],
+            dst_ref=sums.at[my_dp],
+            send_sem=sum_send,
+            recv_sem=sum_recv,
+            device_id=(lax.rem(my_dp + k, n_dp), my_mp),
+            device_id_type=MESH,
+        ).start()
+
+    def late_arrival(g):
+        part = landing.at[0, 0, pl.ds(0, late_each * near)]
+        pltpu.make_async_copy(part, part, late_sem.at[g]).wait()
+
+    @pl.loop(0, late_groups - 1)
+    def _(g):
+        late_arrival(g)
+        turn_late(g)
+        place(late_turned, late_offset.at[g], last_slot)
+
+    late_arrival(late_groups - 1)
+    turn_late(late_groups - 1)
+
+    @pl.loop(0, SLABS // FINAL)
+    def _(j):
+        for u in range(FINAL):
+            s = j * FINAL + u
+            cols = pl.ds(pl.multiple_of(s * slab_rows, slab_rows), slab_rows)
+            found = jnp.dot(late_turned[...], late_onehot[:, cols], preferred_element_type=jnp.float32)
+            block = shards[last_slot : last_slot + PAIR, :, cols].reshape(width, slab_rows) + found.astype(jnp.bfloat16)
+            shards[last_slot : last_slot + PAIR, :, cols] = block.reshape(PAIR, HD, slab_rows)
+            finish(s, block)
+
+    store_checks(last_slot)
     tail_sums[my_dp, :PAIR] = jnp.sum(checks[last_slot : last_slot + PAIR], axis=1)
 
     @pl.loop(1, n_dp)
@@ -297,6 +410,8 @@
     slots = Q_HEADS // n_mp + 2
     chunks = slots // PAIR
     width = PAIR * HD
+    near = n_mp // 4
+    late_rows = near * sub * max(1, HD // (near * sub))
     vmem = pl.BlockSpec(memory_space=pltpu.VMEM)
     hbm = pl.BlockSpec(memory_space=pl.ANY)
     shapes = (
@@ -315,11 +430,13 @@
             pltpu.VMEM((n_mp, rows_dev, width), jnp.float32),
             pltpu.VMEM((2, n_mp, n_dp, sub, width), jnp.bfloat16),
             pltpu.VMEM((width, n_dp * sub), jnp.bfloat16),
-            pltpu.VMEM((width, group_rows), jnp.float32),
             pltpu.VMEM((group_rows, probes), jnp.bfloat16),
             pltpu.VMEM(lane.shape, jnp.bfloat16),
             pltpu.VMEM((n_dev, n_dp, sub), jnp.int32),
             pltpu.VMEM((n_mp, n_dp * sub, HD), jnp.int32),
+            pltpu.VMEM((width, late_rows), jnp.bfloat16),
+            pltpu.VMEM((n_dp * near * sub // late_rows, late_rows, HD), jnp.int32),
+            pltpu.VMEM((late_rows, group_rows), jnp.bfloat16),
             pltpu.VMEM((SLABS, PAIR, probes), jnp.float32),
             pltpu.VMEM((n_dp, slots, probes), jnp.float32),
             pltpu.VMEM((n_dp, 8, probes), jnp.float32),
@@ -328,6 +445,7 @@
             pltpu.SemaphoreType.DMA,
             pltpu.SemaphoreType.DMA((chunks,)),
             pltpu.SemaphoreType.DMA((chunks, n_mp)),
+            pltpu.SemaphoreType.DMA((n_dp * near * sub // late_rows,)),
             pltpu.SemaphoreType.DMA,
             pltpu.SemaphoreType.DMA,
             pltpu.SemaphoreType.DMA,

time: 441 us -> 434 us (0.984)
  Pallas kernels: 440 us -> 433 us
    pallas_call x1, Pallas kernels: 433 us -> 426 us  [body(): pl.pallas_call(functools.partial(exchange, n_dp, n_mp), out_shape=tuple((...]
where the time goes in v2:
time: 434 us
  Pallas kernels  433 us (100%)
    pallas_call x1, Pallas kernels, body(): pl.pallas_call(functools.partial(exchange, n_dp, n_mp), out_shape=tuple((...  426 us

profile of v2, /device:TPU:0, one launch (start us, length us, event | category | flops | bytes accessed | tf_op | source)
XLA Modules:
  0.0 433.7 jit_solution(2851818085522328676)
XLA Ops:
  0.6 426.2 %shard_map.67 = (bf16[18,128,4096]{2,1,0:T(8,128)(2,1)S(1)}, f32[18,8,1024]{2,1,0:T(8,128)S(1)}, f32[18,1024]{1,0:T(8,128)S(1)}, bf16[9,8,4,128,256]{4,3,2,1,0:T(8,128)(2,1)}) custom-call(f32[512,18432]{1,0:T(8,128)} %stored.1, s32[32,4,128]{2,1,0:T(4,128)} %bitcast.1, bf16[4096,1024]{1,0:T(8,128)(2,1)} %probe_any.1, bf16[128,1024]{1,0:T(8,128)(2,1)} %lane_any.1), custom_call_target="tpu_custom_call" | custom-call | tf_op jit(solution)/shard_map/pallas_call | solution.py:422
  426.9 6.8 %shard_map.68 = (bf16[18,128,4096]{2,1,0:T(8,128)(2,1)}, f32[18,8,1024]{2,1,0:T(8,128)}, f32[18,1024]{1,0:T(8,128)}) custom-call(bf16[18,128,4096]{2,1,0:T(8,128)(2,1)S(1)} %get-tuple-element.6.shards, f32[18,8,1024]{2,1,0:T(8,128)S(1)} %get-tuple-element.7.checks, f32[18,1024]{1,0:T(8,128)S(1)} %get-tuple-element.8.heads), custom_call_target="tpu_custom_call" | custom-call | tf_op jit(solution)/shard_map/pallas_call | solution.py:458
